TPU v7x, 32 devices: a whole 2x2x4 slice. The times are simulated.
32 devices in a mesh: dp: 8 (over y, x, core), tensor: 4 (over z).
Axes of the slice: x: 2, y: 2, z: 4, core: 2. Of those that a mesh axis runs over, the one named last changes fastest.
Arguments:
- tokens: bfloat16 [4096, 1024], P(('dp', 'tensor')), may hold values from -5 to 5
- lengths: int32 [8, 2], P('dp'), may hold values from 0 to 512, as said below
- w_query: bfloat16 [1024, 1024], P('dp', 'tensor'), may hold values from -0.1875 to 0.1875
- b_query: float32 [1024], replicated, may hold values from -3 to 3
- w_key: bfloat16 [1024, 1024], P('dp', 'tensor'), may hold values from -0.1875 to 0.1875
- w_value: bfloat16 [1024, 1024], P('dp', 'tensor'), may hold values from -0.1875 to 0.1875
- b_value: float32 [1024], replicated, may hold values from -3 to 3
- w_out: bfloat16 [1024, 1024], P('tensor', 'dp'), may hold values from -3 to 3
- b_out: float32 [1024], replicated, may hold values from -3 to 3
- gain_attn: float32 [1024], replicated, may hold values from 0.1 to 1.9
- shift_attn: float32 [1024], replicated, may hold values from -3 to 3
- w_in: bfloat16 [1024, 4096], P('dp', 'tensor'), may hold values from -0.1875 to 0.1875
- b_in: float32 [4096], replicated, may hold values from -3 to 3
- w_back: bfloat16 [4096, 1024], P('tensor', 'dp'), may hold values from -0.09375 to 0.09375
- b_back: float32 [1024], replicated, may hold values from -3 to 3
- gain_ffn: float32 [1024], replicated, may hold values from 0.1 to 1.9
- shift_ffn: float32 [1024], replicated, may hold values from -3 to 3
- cotangent: bfloat16 [4096, 1024], P(('dp', 'tensor')), may hold values from -6 to 6
Outputs:
- output: bfloat16 [4096, 1024], P(('dp', 'tensor'))
- grad_tokens: float32 [4096, 1024], P(('dp', 'tensor'))
- grad_w_query: float32 [1024, 1024], P('dp', 'tensor')
- grad_b_query: float32 [1024], replicated
- grad_w_key: float32 [1024, 1024], P('dp', 'tensor')
- grad_w_value: float32 [1024, 1024], P('dp', 'tensor')
- grad_b_value: float32 [1024], replicated
- grad_w_out: float32 [1024, 1024], P('tensor', 'dp')
- grad_b_out: float32 [1024], replicated
- grad_gain_attn: float32 [1024], replicated
- grad_shift_attn: float32 [1024], replicated
- grad_w_in: float32 [1024, 4096], P('dp', 'tensor')
- grad_b_in: float32 [4096], replicated
- grad_w_back: float32 [4096, 1024], P('tensor', 'dp')
- grad_b_back: float32 [1024], replicated
- grad_gain_ffn: float32 [1024], replicated
- grad_shift_ffn: float32 [1024], replicated
Inputs may be any that keep to these rules, and one draw needn't show every extreme that they name: Each group's 2 lengths sum to at most 512; the first is 1 or more, the second may be 0; in every draw one group holds a single sequence of exactly 512 tokens.
All inputs are finite; a program needn't handle non-finite values.
Results may differ from a plain program's by a relative error of at most 0.02.
Values may be sent and summed in bfloat16 or wider, within the bound.
A program may use at most 128 MiB of HBM per device.

v0:
```python
import jax
import jax.numpy as jnp
from jax import lax
from jax.sharding import PartitionSpec as P

HD = 64
epsilon = 1e-06
masked_value = -1e30


def matmul_plain(left_side, right_side):
    return jnp.dot(left_side, right_side, preferred_element_type=jnp.float32)


def matmul_over_rows(left_side, right_side):
    return lax.dot_general(
        left_side, right_side, (((0,), (0,)), ((), ())), preferred_element_type=jnp.float32
    )


def matmul_over_cols(left_side, right_side):
    return lax.dot_general(
        left_side, right_side, (((1,), (1,)), ((), ())), preferred_element_type=jnp.float32
    )


def layer_norm(residual, gain_vec, shift_vec):
    mean_val = jnp.mean(residual, axis=-1, keepdims=True)
    centered = residual - mean_val
    inv_std = lax.rsqrt(jnp.mean(centered * centered, axis=-1, keepdims=True) + epsilon)
    normed = centered * inv_std
    return (normed * gain_vec + shift_vec, normed, inv_std)


def norm_back(grad_out, normed, inv_std, gain_vec):
    grad_norm = grad_out * gain_vec
    first_mean = jnp.mean(grad_norm, axis=-1, keepdims=True)
    second_mean = jnp.mean(grad_norm * normed, axis=-1, keepdims=True)
    return inv_std * (grad_norm - first_mean - normed * second_mean)


def gelu_parts(preact):
    cdf_val = 0.5 * (1.0 + lax.erf(preact * 0.7071067811865476))
    pdf_val = jnp.exp(-0.5 * preact * preact) * 0.3989422804014327
    return (preact * cdf_val, cdf_val + preact * pdf_val)


def attend_forward(query_rows, key_rows, value_rows, seg_ids, head_dim, block_rows):
    group_rows, head_cols = query_rows.shape
    pair_width = 2 * head_dim
    block_count = group_rows // block_rows
    pair_count = head_cols // pair_width
    score_scale = head_dim ** (-0.5)

    def attend_step(step_index, loop_carry):
        context, log_total = loop_carry
        pair_index = step_index // block_count
        row_start = step_index % block_count * block_rows
        first_col = pair_index * pair_width
        query_block = lax.dynamic_slice(
            query_rows, (row_start, first_col), (block_rows, pair_width)
        ).reshape(block_rows, 2, head_dim)
        key_pair = lax.dynamic_slice(key_rows, (0, first_col), (group_rows, pair_width)).reshape(
            group_rows, 2, head_dim
        )
        value_pair = lax.dynamic_slice(
            value_rows, (0, first_col), (group_rows, pair_width)
        ).reshape(group_rows, 2, head_dim)
        same_seg = seg_ids[:, None] == seg_ids[None, :]
        scores = (
            jnp.einsum("qhd,khd->hqk", query_block, key_pair, preferred_element_type=jnp.float32)
            * score_scale
        )
        scores = jnp.where(same_seg[None], scores, masked_value)
        row_max = jnp.max(scores, axis=-1, keepdims=True)
        block_total = row_max + jnp.log(jnp.sum(jnp.exp(scores - row_max), axis=-1, keepdims=True))
        prob_bf = jnp.exp(scores - block_total).astype(jnp.bfloat16)
        context_block = jnp.einsum(
            "hqk,khd->qhd", prob_bf, value_pair, preferred_element_type=jnp.float32
        ).astype(jnp.bfloat16)
        context = lax.dynamic_update_slice(
            context, context_block.reshape(block_rows, pair_width), (row_start, first_col)
        )
        log_total = lax.dynamic_update_slice(
            log_total, block_total[:, :, 0], (2 * pair_index, row_start)
        )
        return (context, log_total)

    start_carry = (
        jnp.zeros((group_rows, head_cols), jnp.bfloat16),
        jnp.zeros((head_cols // head_dim, group_rows), jnp.float32),
    )
    return lax.fori_loop(0, pair_count * block_count, attend_step, start_carry)


def attend_backward(
    query_rows,
    key_rows,
    value_rows,
    context,
    grad_context,
    log_total,
    seg_ids,
    head_dim,
    block_rows,
):
    group_rows, head_cols = query_rows.shape
    pair_width = 2 * head_dim
    block_count = group_rows // block_rows
    pair_count = head_cols // pair_width
    score_scale = head_dim ** (-0.5)

    def back_step(step_index, loop_carry):
        grad_query, grad_keys, grad_values = loop_carry
        pair_index = step_index // block_count
        row_start = step_index % block_count * block_rows
        first_col = pair_index * pair_width
        query_block = lax.dynamic_slice(
            query_rows, (row_start, first_col), (block_rows, pair_width)
        ).reshape(block_rows, 2, head_dim)
        key_pair = lax.dynamic_slice(key_rows, (0, first_col), (group_rows, pair_width)).reshape(
            group_rows, 2, head_dim
        )
        value_pair = lax.dynamic_slice(
            value_rows, (0, first_col), (group_rows, pair_width)
        ).reshape(group_rows, 2, head_dim)
        context_block = lax.dynamic_slice(
            context, (row_start, first_col), (block_rows, pair_width)
        ).reshape(block_rows, 2, head_dim)
        gctx_block = lax.dynamic_slice(
            grad_context, (row_start, first_col), (block_rows, pair_width)
        ).reshape(block_rows, 2, head_dim)
        total_block = lax.dynamic_slice(log_total, (2 * pair_index, row_start), (2, block_rows))
        same_seg = seg_ids[:, None] == seg_ids[None, :]
        scores = (
            jnp.einsum("qhd,khd->hqk", query_block, key_pair, preferred_element_type=jnp.float32)
            * score_scale
        )
        scores = jnp.where(same_seg[None], scores, masked_value)
        probs = jnp.exp(scores - total_block[:, :, None])
        prob_bf = probs.astype(jnp.bfloat16)
        grad_probs = jnp.einsum(
            "qhd,khd->hqk", gctx_block, value_pair, preferred_element_type=jnp.float32
        )
        delta_rows = jnp.sum(
            gctx_block.astype(jnp.float32) * context_block.astype(jnp.float32), axis=-1
        ).T[:, :, None]
        grad_scores = (probs * (grad_probs - delta_rows) * score_scale).astype(jnp.bfloat16)
        grad_q_block = jnp.einsum(
            "hqk,khd->qhd", grad_scores, key_pair, preferred_element_type=jnp.float32
        ).reshape(block_rows, pair_width)
        grad_k_pair = jnp.einsum(
            "hqk,qhd->khd", grad_scores, query_block, preferred_element_type=jnp.float32
        ).reshape(group_rows, pair_width)
        grad_v_pair = jnp.einsum(
            "hqk,qhd->khd", prob_bf, gctx_block, preferred_element_type=jnp.float32
        ).reshape(group_rows, pair_width)
        grad_query = lax.dynamic_update_slice(grad_query, grad_q_block, (row_start, first_col))
        old_keys = lax.dynamic_slice(grad_keys, (0, first_col), (group_rows, pair_width))
        grad_keys = lax.dynamic_update_slice(grad_keys, old_keys + grad_k_pair, (0, first_col))
        old_values = lax.dynamic_slice(grad_values, (0, first_col), (group_rows, pair_width))
        grad_values = lax.dynamic_update_slice(
            grad_values, old_values + grad_v_pair, (0, first_col)
        )
        return (grad_query, grad_keys, grad_values)

    zero_grad = jnp.zeros((group_rows, head_cols), jnp.float32)
    return lax.fori_loop(0, pair_count * block_count, back_step, (zero_grad, zero_grad, zero_grad))


def on_device(
    tokens,
    lengths,
    w_query,
    b_query,
    w_key,
    w_value,
    b_value,
    w_out,
    b_out,
    gain_attn,
    shift_attn,
    w_in,
    b_in,
    w_back,
    b_back,
    gain_ffn,
    shift_ffn,
    cotangent,
):
    tensor_size = lax.axis_size("tensor")
    tensor_index = lax.axis_index("tensor")
    local_rows = tokens.shape[0]
    group_rows = local_rows * tensor_size
    head_cols = w_query.shape[1]
    hidden_cols = w_in.shape[1]
    block_rows = min(512, group_rows)
    seq_lens = lengths[0]
    live_end = seq_lens[0] + seq_lens[1]
    positions = jnp.arange(group_rows, dtype=jnp.int32)
    seg_ids = (positions >= seq_lens[0]).astype(jnp.int32) + (positions >= live_end).astype(
        jnp.int32
    )
    local_pos = tensor_index * local_rows + jnp.arange(local_rows, dtype=jnp.int32)
    live_rows = (local_pos < live_end).astype(jnp.float32)[:, None]
    rows_full = lax.all_gather(tokens, "tensor", axis=0, tiled=True)
    attn_mats = (
        lax.all_gather(w_query, "dp", axis=0, tiled=True),
        lax.all_gather(w_key, "dp", axis=0, tiled=True),
        lax.all_gather(w_value, "dp", axis=0, tiled=True),
        lax.all_gather(w_out, "dp", axis=1, tiled=True),
    )
    mat_query, mat_key, mat_value, mat_out = attn_mats
    bias_query = lax.dynamic_slice_in_dim(b_query, tensor_index * head_cols, head_cols)
    bias_value = lax.dynamic_slice_in_dim(b_value, tensor_index * head_cols, head_cols)
    bias_in = lax.dynamic_slice_in_dim(b_in, tensor_index * hidden_cols, hidden_cols)
    query_rows = (matmul_plain(rows_full, mat_query) + bias_query).astype(jnp.bfloat16)
    key_rows = matmul_plain(rows_full, mat_key).astype(jnp.bfloat16)
    value_rows = (matmul_plain(rows_full, mat_value) + bias_value).astype(jnp.bfloat16)
    context, log_total = attend_forward(query_rows, key_rows, value_rows, seg_ids, HD, block_rows)
    attn_sum = lax.psum_scatter(
        matmul_plain(context, mat_out).astype(jnp.bfloat16),
        "tensor",
        scatter_dimension=0,
        tiled=True,
    ).astype(jnp.float32)
    resid_one = tokens.astype(jnp.float32) + attn_sum + b_out
    hidden_one, normed_one, inv_one = layer_norm(resid_one, gain_attn, shift_attn)
    hidden_bf = hidden_one.astype(jnp.bfloat16)
    hidden_full = lax.all_gather(hidden_bf, "tensor", axis=0, tiled=True)
    ffn_mats = (
        lax.all_gather(w_in, "dp", axis=0, tiled=True),
        lax.all_gather(w_back, "dp", axis=1, tiled=True),
    )
    mat_in, mat_back = ffn_mats
    preact = matmul_plain(hidden_full, mat_in) + bias_in
    activ_val, gelu_slope = gelu_parts(preact)
    activation = activ_val.astype(jnp.bfloat16)
    ffn_sum = lax.psum_scatter(
        matmul_plain(activation, mat_back).astype(jnp.bfloat16),
        "tensor",
        scatter_dimension=0,
        tiled=True,
    ).astype(jnp.float32)
    resid_two = hidden_one + ffn_sum + b_back
    normed_out, normed_two, inv_two = layer_norm(resid_two, gain_ffn, shift_ffn)
    output = (normed_out * live_rows).astype(jnp.bfloat16)
    grad_final = cotangent.astype(jnp.float32) * live_rows
    grad_gain_ffn = jnp.sum(grad_final * normed_two, axis=0)
    grad_shift_ffn = jnp.sum(grad_final, axis=0)
    grad_two = norm_back(grad_final, normed_two, inv_two, gain_ffn)
    grad_b_back = jnp.sum(grad_two, axis=0)
    mat_query, mat_key, mat_value, mat_out, mat_in, mat_back = (
        lax.all_gather(w_query, "dp", axis=0, tiled=True),
        lax.all_gather(w_key, "dp", axis=0, tiled=True),
        lax.all_gather(w_value, "dp", axis=0, tiled=True),
        lax.all_gather(w_out, "dp", axis=1, tiled=True),
        lax.all_gather(w_in, "dp", axis=0, tiled=True),
        lax.all_gather(w_back, "dp", axis=1, tiled=True),
    )
    grad_two_full = lax.all_gather(grad_two.astype(jnp.bfloat16), "tensor", axis=0, tiled=True)
    grad_w_back = matmul_over_rows(activation, grad_two_full)
    grad_pre = matmul_over_cols(grad_two_full, mat_back) * gelu_slope
    grad_b_in_part = jnp.sum(grad_pre, axis=0)
    grad_pre_bf = grad_pre.astype(jnp.bfloat16)
    grad_w_in = matmul_over_rows(hidden_full, grad_pre_bf)
    grad_one_out = grad_two + lax.psum_scatter(
        matmul_over_cols(grad_pre_bf, mat_in).astype(jnp.bfloat16),
        "tensor",
        scatter_dimension=0,
        tiled=True,
    ).astype(jnp.float32)
    grad_w_in, grad_w_back = (
        lax.psum_scatter(grad_w_in, "dp", scatter_dimension=0, tiled=True),
        lax.psum_scatter(grad_w_back, "dp", scatter_dimension=1, tiled=True),
    )
    grad_gain_attn = jnp.sum(grad_one_out * normed_one, axis=0)
    grad_shift_attn = jnp.sum(grad_one_out, axis=0)
    grad_one = norm_back(grad_one_out, normed_one, inv_one, gain_attn)
    grad_b_out = jnp.sum(grad_one, axis=0)
    grad_one_full = lax.all_gather(grad_one.astype(jnp.bfloat16), "tensor", axis=0, tiled=True)
    grad_w_out = matmul_over_rows(context, grad_one_full)
    grad_context = matmul_over_cols(grad_one_full, mat_out).astype(jnp.bfloat16)
    grad_query, grad_keys, grad_values = attend_backward(
        query_rows, key_rows, value_rows, context, grad_context, log_total, seg_ids, HD, block_rows
    )
    grad_b_query_part = jnp.sum(grad_query, axis=0)
    grad_b_value_part = jnp.sum(grad_values, axis=0)
    grad_query_bf = grad_query.astype(jnp.bfloat16)
    grad_keys_bf = grad_keys.astype(jnp.bfloat16)
    grad_values_bf = grad_values.astype(jnp.bfloat16)
    grad_w_query = matmul_over_rows(rows_full, grad_query_bf)
    grad_w_key = matmul_over_rows(rows_full, grad_keys_bf)
    grad_w_value = matmul_over_rows(rows_full, grad_values_bf)
    query_part = matmul_over_cols(grad_query_bf, mat_query)
    key_part = matmul_over_cols(grad_keys_bf, mat_key)
    value_part = matmul_over_cols(grad_values_bf, mat_value)
    grad_in = grad_one + lax.psum_scatter(
        (query_part + key_part + value_part).astype(jnp.bfloat16),
        "tensor",
        scatter_dimension=0,
        tiled=True,
    ).astype(jnp.float32)
    grad_w_query, grad_w_key, grad_w_value, grad_w_out = (
        lax.psum_scatter(grad_w_query, "dp", scatter_dimension=0, tiled=True),
        lax.psum_scatter(grad_w_key, "dp", scatter_dimension=0, tiled=True),
        lax.psum_scatter(grad_w_value, "dp", scatter_dimension=0, tiled=True),
        lax.psum_scatter(grad_w_out, "dp", scatter_dimension=1, tiled=True),
    )

    def widen(part_vec, full_width):
        return lax.dynamic_update_slice_in_dim(
            jnp.zeros((full_width,), jnp.float32), part_vec, tensor_index * part_vec.shape[0], 0
        )

    small_sums = lax.psum(
        (
            widen(grad_b_query_part, b_query.shape[0]),
            widen(grad_b_value_part, b_value.shape[0]),
            grad_b_out,
            grad_gain_attn,
            grad_shift_attn,
            widen(grad_b_in_part, b_in.shape[0]),
            grad_b_back,
            grad_gain_ffn,
            grad_shift_ffn,
        ),
        ("dp", "tensor"),
    )
    return (
        output,
        grad_in,
        grad_w_query,
        small_sums[0],
        grad_w_key,
        grad_w_value,
        small_sums[1],
        grad_w_out,
        small_sums[2],
        small_sums[3],
        small_sums[4],
        grad_w_in,
        small_sums[5],
        grad_w_back,
        small_sums[6],
        small_sums[7],
        small_sums[8],
    )


def solution(mesh):
    placed = (
        P(("dp", "tensor"), None),
        P("dp", None),
        P("dp", "tensor"),
        P(),
        P("dp", "tensor"),
        P("dp", "tensor"),
        P(),
        P("tensor", "dp"),
        P(),
        P(),
        P(),
        P("dp", "tensor"),
        P(),
        P("tensor", "dp"),
        P(),
        P(),
        P(),
        P(("dp", "tensor"), None),
    )
    return jax.shard_map(
        on_device,
        mesh=mesh,
        in_specs=placed,
        out_specs=(
            P(("dp", "tensor"), None),
            P(("dp", "tensor"), None),
            P("dp", "tensor"),
            P(),
            P("dp", "tensor"),
            P("dp", "tensor"),
            P(),
            P("tensor", "dp"),
            P(),
            P(),
            P(),
            P("dp", "tensor"),
            P(),
            P("tensor", "dp"),
            P(),
            P(),
            P(),
        ),
        check_vma=False,
    )
```

profile of v0, /device:TPU:0, one launch (start us, length us, event | category | flops | bytes accessed | tf_op | source)
XLA Modules:
  0.0 598.6 jit_solution(13437722508312491656)
XLA Ops:
  13.0 11.6 %all_gather.37 = bf16[1024,256]{1,0:T(8,128)(2,1)S(1)} all-gather(bf16[128,256]{1,0:T(8,128)(2,1)} %param.27), channel_id=1, replica_groups=mesh['dp'=8,'tensor'=4] {'dp'}, dimensions={0}, use_global_device_ids=true | all-gather | bytes 589824 | tf_op jit(solution)/shard_map/all_gather | solution.py:210
  24.6 9.5 %all_gather.38 = bf16[1024,256]{1,0:T(8,128)(2,1)S(1)} all-gather(bf16[128,256]{1,0:T(8,128)(2,1)} %param.24), channel_id=1, replica_groups=mesh['dp'=8,'tensor'=4] {'dp'}, dimensions={0}, use_global_device_ids=true | all-gather | bytes 589824 | tf_op jit(solution)/shard_map/all_gather | solution.py:208
  34.1 9.2 %all_gather.39 = bf16[1024,256]{1,0:T(8,128)(2,1)S(1)} all-gather(bf16[128,256]{1,0:T(8,128)(2,1)} %param.26), channel_id=1, replica_groups=mesh['dp'=8,'tensor'=4] {'dp'}, dimensions={0}, use_global_device_ids=true | all-gather | bytes 589824 | tf_op jit(solution)/shard_map/all_gather | solution.py:209
  43.3 10.6 %all_gather.40 = bf16[256,1024]{1,0:T(8,128)(2,1)} all-gather(bf16[256,128]{1,0:T(8,128)(2,1)S(1)} %copy-done.33), channel_id=1, replica_groups=mesh['dp'=8,'tensor'=4] {'dp'}, dimensions={1}, use_global_device_ids=true | all-gather | bytes 589824 | tf_op jit(solution)/shard_map/all_gather | solution.py:211
  57.1 4.8 while.38
  61.9 2.5 convolution_convert_fusion.3
  65.1 27.1 %reduce-scatter.11.cloned.1.call-done = bf16[128,1024]{1,0:T(8,128)(2,1)} async-done(((bf16[512,1024]{1,0:T(8,128)(2,1)}), bf16[128,1024]{1,0:T(8,128)(2,1)}) %reduce-scatter.11.cloned.1.call-update) | async-done | bytes 262160 | tf_op jit(solution)/shard_map/reduce_scatter | solution.py:221
  94.5 1.8 fusion.21
  97.6 27.1 %all-gather.9.cloned.1.call-done = bf16[512,1024]{1,0:T(8,128)(2,1)} async-done(((bf16[128,1024]{1,0:T(8,128)(2,1)}), bf16[512,1024]{1,0:T(8,128)(2,1)}) %all-gather.9.cloned.1.call-update) | async-done | bytes 1048592 | tf_op jit(solution)/shard_map/all_gather | solution.py:230
  124.7 4.6 multiply_convert_fusion.1
  129.3 24.4 %all-gather.13.cloned.1.call-done = bf16[1024,1024]{1,0:T(8,128)(2,1)} async-done(((bf16[1024,128]{1,0:T(8,128)(2,1)}), bf16[1024,1024]{1,0:T(8,128)(2,1)}) %all-gather.13.cloned.1.call-update) | async-done | bytes 2097168 | tf_op jit(solution)/shard_map/all_gather | solution.py:233
  153.8 3.9 convolution_convert_fusion.2
  157.7 27.4 %reduce-scatter.13.cloned.1.call-done = bf16[128,1024]{1,0:T(8,128)(2,1)} async-done(((bf16[512,1024]{1,0:T(8,128)(2,1)}), bf16[128,1024]{1,0:T(8,128)(2,1)}) %reduce-scatter.13.cloned.1.call-update) | async-done | bytes 262160 | tf_op jit(solution)/shard_map/reduce_scatter | solution.py:239
  188.3 26.4 %all-gather.15.cloned.1.call-done = bf16[512,1024]{1,0:T(8,128)(2,1)} async-done(((bf16[128,1024]{1,0:T(8,128)(2,1)}), bf16[512,1024]{1,0:T(8,128)(2,1)}) %all-gather.15.cloned.1.call-update) | async-done | bytes 1048592 | tf_op jit(solution)/shard_map/all_gather | solution.py:261
  214.7 5.2 fusion.37
  220.9 2.3 convolution_convert_fusion.1
  223.3 26.8 %reduce-scatter.15.cloned.1.call-done = bf16[128,1024]{1,0:T(8,128)(2,1)} async-done(((bf16[512,1024]{1,0:T(8,128)(2,1)}), bf16[128,1024]{1,0:T(8,128)(2,1)}) %reduce-scatter.15.cloned.1.call-update) | async-done | bytes 262160 | tf_op jit(solution)/shard_map/reduce_scatter | solution.py:267
  250.0 2.0 multiply_reduce_fusion.1
  252.0 1.8 fusion.32
  254.7 26.5 %all-gather.17.cloned.1.call-done = bf16[512,1024]{1,0:T(8,128)(2,1)} async-done(((bf16[128,1024]{1,0:T(8,128)(2,1)}), bf16[512,1024]{1,0:T(8,128)(2,1)}) %all-gather.17.cloned.1.call-update) | async-done | bytes 1048592 | tf_op jit(solution)/shard_map/all_gather | solution.py:281
  281.2 2.4 convolution_convert_fusion.4
  284.6 13.1 %while.39 = (s32[]{:T(128)}, f32[512,256]{0,1:T(8,128)}, f32[512,256]{0,1:T(8,128)S(1)}, f32[512,256]{0,1:T(8,128)S(1)}, bf16[512,256]{0,1:T(8,128)(2,1)S(1)}, /...) while((s32[]{:T(128)}, f32[512,256]{0,1:T(8,128)}, ...), condition=%wide.region_17.18_spmd.clone, body=%wide.region_15.17_spmd.clone.sunk | while | flops 340395520 | bytes 25846364 | solution.py:168
  297.7 2.9 convolution_bitcast_fusion.2
  309.5 4.5 fusion.41
  315.5 3.3 fusion.15
  321.4 41.4 %all-reduce = (f32[1024]{0:T(1024)}, f32[1024]{0:T(1024)}, f32[1024]{0:T(1024)}, f32[1024]{0:T(1024)}, f32[1024]{0:T(1024)}, /*index=5*/f32[4096]{0:T(1024)}, f32[1024]{0:T(1024)}, f32[1024]{0:T(1024)}, f32[1024]{0:T(1024)}) all-reduce(f32[1024]{0:T(1024)S(1)} %dynamic_update_slice.62, ...), channel_id=1, replica_groups=mesh['dp'=8,'tensor'=4] {'dp','tensor'}, use_global_device_ids=true, to_apply=%region_21.22 | all-reduce | flops 12288 | bytes 98304 | tf_op jit(solution)/shard_map/psum | solution.py:316
  364.4 10.7 %reduce-scatter.21.cloned.1.call-done = f32[128,256]{0,1:T(8,128)} async-done(((f32[1024,256]{0,1:T(8,128)}), f32[128,256]{0,1:T(8,128)}) %reduce-scatter.21.cloned.1.call-update) | async-done | bytes 131088 | tf_op jit(solution)/shard_map/reduce_scatter | solution.py:306
  376.8 37.3 %reduce-scatter.23.cloned.1.call-done = f32[128,256]{0,1:T(8,128)} async-done(((f32[1024,256]{0,1:T(8,128)}), f32[128,256]{0,1:T(8,128)}) %reduce-scatter.23.cloned.1.call-update) | async-done | bytes 131088 | tf_op jit(solution)/shard_map/reduce_scatter | solution.py:307
  415.8 27.8 %reduce-scatter.17.cloned.1.call-done = bf16[128,1024]{1,0:T(8,128)(2,1)} async-done(((bf16[512,1024]{1,0:T(8,128)(2,1)}), bf16[128,1024]{1,0:T(8,128)(2,1)}) %reduce-scatter.17.cloned.1.call-update) | async-done | bytes 262160 | tf_op jit(solution)/shard_map/reduce_scatter | solution.py:298
  445.4 36.2 %reduce-scatter.25.cloned.1.call-done = f32[256,128]{1,0:T(8,128)} async-done(((f32[256,1024]{1,0:T(8,128)}), f32[256,128]{1,0:T(8,128)}) %reduce-scatter.25.cloned.1.call-update) | async-done | bytes 131088 | tf_op jit(solution)/shard_map/reduce_scatter | solution.py:308
  481.6 54.9 %reduce-scatter.29.cloned.1.call-done = f32[1024,128]{1,0:T(8,128)} async-done(((f32[1024,1024]{1,0:T(8,128)}), f32[1024,128]{1,0:T(8,128)}) %reduce-scatter.29.cloned.1.call-update) | async-done | bytes 524304 | tf_op jit(solution)/shard_map/reduce_scatter | solution.py:275
  536.5 54.8 %reduce-scatter.27.cloned.1.call-done = f32[128,1024]{1,0:T(8,128)} async-done(((f32[1024,1024]{1,0:T(8,128)}), f32[128,1024]{1,0:T(8,128)}) %reduce-scatter.27.cloned.1.call-update) | async-done | bytes 524304 | tf_op jit(solution)/shard_map/reduce_scatter | solution.py:274
  (243 shorter events, 53.9 us)
Async XLA Ops:
  8.0 35.3 %copy-start.33 = (bf16[256,128]{1,0:T(8,128)(2,1)S(1)}, bf16[256,128]{1,0:T(8,128)(2,1)}, u32[]{:S(2)}) copy-start(bf16[256,128]{1,0:T(8,128)(2,1)} %param.29) | copy-start | bytes 196612
  8.0 45.8 %all-gather.7.cloned.1.call-start = ((), (), s32[]{:S(2)}) async-start(), calls=%async_computation.10 | async-start | bytes 1310720 | tf_op jit(solution)/shard_map/all_gather | solution.py:206
  8.8 83.4 %reduce-scatter.11.cloned.1.call-start = ((), (), s32[]{:S(2)}) async-start(), calls=%async_computation.11 | async-start | bytes 1310720 | tf_op jit(solution)/shard_map/reduce_scatter | solution.py:221
  24.6 31.2 %copy-start.16 = (bf16[1024,256]{1,0:T(8,128)(2,1)}, bf16[1024,256]{1,0:T(8,128)(2,1)S(1)}, u32[]{:S(2)}) copy-start(bf16[1024,256]{1,0:T(8,128)(2,1)S(1)} %all_gather.37) | copy-start | bytes 1572868
  34.1 22.2 %copy-start.19 = (bf16[1024,256]{1,0:T(8,128)(2,1)}, bf16[1024,256]{1,0:T(8,128)(2,1)S(1)}, u32[]{:S(2)}) copy-start(bf16[1024,256]{1,0:T(8,128)(2,1)S(1)} %all_gather.38) | copy-start | bytes 1572868
  61.8 30.3 %copy-start.2 = (bf16[128,1024]{1,0:T(8,128)(2,1)S(1)}, bf16[128,1024]{1,0:T(8,128)(2,1)}, u32[]{:S(2)}) copy-start(bf16[128,1024]{1,0:T(8,128)(2,1)} %param.22) | copy-start | bytes 786436
  61.9 30.3 %copy-start.31 = (f32[1024]{0:T(1024)S(1)}, f32[1024]{0:T(1024)}, u32[]{:S(2)}) copy-start(f32[1024]{0:T(1024)} %param.30) | copy-start | bytes 12292
  61.9 32.6 %copy-start.32 = (f32[1024]{0:T(1024)S(1)}, f32[1024]{0:T(1024)}, u32[]{:S(2)}) copy-start(f32[1024]{0:T(1024)} %param.31) | copy-start | bytes 12292
  61.9 32.6 %copy-start.34 = (f32[1024]{0:T(1024)S(1)}, f32[1024]{0:T(1024)}, u32[]{:S(2)}) copy-start(f32[1024]{0:T(1024)} %param.32) | copy-start | bytes 12292
  64.4 33.2 %all-gather.11.cloned.1.call-start = ((), (), s32[]{:S(2)}) async-start(), calls=%async_computation.13 | async-start | bytes 2359296 | tf_op jit(solution)/shard_map/all_gather | solution.py:232
  65.0 59.7 %all-gather.9.cloned.1.call-start = ((), (), s32[]{:S(2)}) async-start(), calls=%async_computation.12 | async-start | bytes 1310720 | tf_op jit(solution)/shard_map/all_gather | solution.py:230
  96.3 57.5 %all-gather.13.cloned.1.call-start = ((), (), s32[]{:S(2)}) async-start(), calls=%async_computation.14 | async-start | bytes 2359296 | tf_op jit(solution)/shard_map/all_gather | solution.py:233
  96.9 88.2 %reduce-scatter.13.cloned.1.call-start = ((), (), s32[]{:S(2)}) async-start(), calls=%async_computation.15 | async-start | bytes 1310720 | tf_op jit(solution)/shard_map/reduce_scatter | solution.py:239
  129.3 28.3 %copy-start.25 = (bf16[512,1024]{1,0:T(8,128)(2,1)}, bf16[512,1024]{1,0:T(8,128)(2,1)S(1)}, u32[]{:S(2)}) copy-start(bf16[512,1024]{1,0:T(8,128)(2,1)S(1)} %get-tuple-element.629) | copy-start | bytes 3145732
  153.8 31.3 %copy-start.11 = (bf16[128,1024]{1,0:T(8,128)(2,1)S(1)}, bf16[128,1024]{1,0:T(8,128)(2,1)}, u32[]{:S(2)}) copy-start(bf16[128,1024]{1,0:T(8,128)(2,1)} %reduce-scatter.11.cloned.1.call-done) | copy-start | bytes 786436
  153.8 31.3 %copy-start.40 = (f32[1024]{0:T(1024)S(1)}, f32[1024]{0:T(1024)}, u32[]{:S(2)}) copy-start(f32[1024]{0:T(1024)} %param.36) | copy-start | bytes 12292
  157.6 29.0 %copy-start.28 = (bf16[128,1024]{1,0:T(8,128)(2,1)S(1)}, bf16[128,1024]{1,0:T(8,128)(2,1)}, u32[]{:S(2)}) copy-start(bf16[128,1024]{1,0:T(8,128)(2,1)} %param.39) | copy-start | bytes 786436
  157.6 29.0 %copy-start.35 = (f32[1024]{0:T(1024)S(1)}, f32[1024]{0:T(1024)}, u32[]{:S(2)}) copy-start(f32[1024]{0:T(1024)} %param.37) | copy-start | bytes 12292
  157.6 29.4 %copy-start.41 = (f32[1024]{0:T(1024)S(1)}, f32[1024]{0:T(1024)}, u32[]{:S(2)}) copy-start(f32[1024]{0:T(1024)} %param.38) | copy-start | bytes 12292
  157.7 57.1 %all-gather.15.cloned.1.call-start = ((), (), s32[]{:S(2)}) async-start(), calls=%async_computation.16 | async-start | bytes 1310720 | tf_op jit(solution)/shard_map/all_gather | solution.py:261
  188.1 61.9 %reduce-scatter.15.cloned.1.call-start = ((), (), s32[]{:S(2)}) async-start(), calls=%async_computation.17 | async-start | bytes 1310720 | tf_op jit(solution)/shard_map/reduce_scatter | solution.py:267
  223.2 58.0 %all-gather.17.cloned.1.call-start = ((), (), s32[]{:S(2)}) async-start(), calls=%async_computation.18 | async-start | bytes 1310720 | tf_op jit(solution)/shard_map/all_gather | solution.py:281
  250.0 31.2 %copy-start.18 = (bf16[256,1024]{1,0:T(8,128)(2,1)S(1)}, bf16[256,1024]{1,0:T(8,128)(2,1)}, u32[]{:S(2)}) copy-start(bf16[256,1024]{1,0:T(8,128)(2,1)} %all_gather.40) | copy-start | bytes 1572868
  253.8 29.8 %copy-start.14 = (f32[128,1024]{1,0:T(8,128)}, f32[128,1024]{1,0:T(8,128)S(1)}, u32[]{:S(2)}) copy-start(f32[128,1024]{1,0:T(8,128)S(1)} %get-tuple-element.615) | copy-start | bytes 1572868
  254.7 108.1 %reduce-scatter.19.cloned.1.call-start = ((), (), s32[]{:S(2)}) async-start(), calls=%async_computation.20 | async-start | bytes 1179648 | tf_op jit(solution)/shard_map/reduce_scatter | solution.py:305
  300.6 74.5 %reduce-scatter.21.cloned.1.call-start = ((), (), s32[]{:S(2)}) async-start(), calls=%async_computation.21 | async-start | bytes 1179648 | tf_op jit(solution)/shard_map/reduce_scatter | solution.py:306
  302.2 111.9 %reduce-scatter.23.cloned.1.call-start = ((), (), s32[]{:S(2)}) async-start(), calls=%async_computation.22 | async-start | bytes 1179648 | tf_op jit(solution)/shard_map/reduce_scatter | solution.py:307
  303.7 139.8 %reduce-scatter.17.cloned.1.call-start = ((), (), s32[]{:S(2)}) async-start(), calls=%async_computation.19 | async-start | bytes 1310720 | tf_op jit(solution)/shard_map/reduce_scatter | solution.py:298
  307.9 173.7 %reduce-scatter.25.cloned.1.call-start = ((), (), s32[]{:S(2)}) async-start(), calls=%async_computation.23 | async-start | bytes 1179648 | tf_op jit(solution)/shard_map/reduce_scatter | solution.py:308
  309.4 227.1 %reduce-scatter.29.cloned.1.call-start = ((), (), s32[]{:S(2)}) async-start(), calls=%async_computation.25 | async-start | bytes 4718592 | tf_op jit(solution)/shard_map/reduce_scatter | solution.py:275
  314.0 277.3 %reduce-scatter.27.cloned.1.call-start = ((), (), s32[]{:S(2)}) async-start(), calls=%async_computation.24 | async-start | bytes 4718592 | tf_op jit(solution)/shard_map/reduce_scatter | solution.py:274
  318.8 124.8 %copy-start.15 = (f32[128,1024]{1,0:T(8,128)S(1)}, f32[128,1024]{1,0:T(8,128)}, u32[]{:S(2)}) copy-start(f32[128,1024]{1,0:T(8,128)} %copy-done.14) | copy-start | bytes 1572868
  (39 other events, 77.4 us)
Sparse Core Ops, SparseCore 0:
  10.4 30.6 all-gather.6
  64.5 27.5 reduce-scatter.10
  157.8 27.2 reduce-scatter.12
  188.2 26.4 all-gather.14
  223.3 26.6 reduce-scatter.14
Sparse Core Ops, SparseCore 1:
  66.8 27.9 all-gather.10
  96.8 27.9 all-gather.8
  126.4 27.3 all-gather.12
  254.7 26.4 all-gather.16
  300.7 35.2 reduce-scatter.18
  339.2 35.9 reduce-scatter.20
  378.2 35.9 reduce-scatter.22
  416.3 27.2 reduce-scatter.16
  447.2 34.3 reduce-scatter.24
  485.5 50.9 reduce-scatter.28
  540.3 50.9 reduce-scatter.26
where the time goes:
time: 600 us; the launch traced here: 599 us
  waiting for transfers between devices  409 us (68%)
  blocking collectives  82.3 us (14%)
  matrix products  48.7 us (8%)
  other arithmetic  21.4 us (4%)
  local copies, waits for them, and re-layouts  17.9 us (3%)
  between operations  17.3 us (3%)
    reduce_scatter x1, waiting for transfers between devices, on_device(): lax.psum_scatter(grad_w_back, 'dp', scatter_dimension=1, tiled=True)  54.9 us
    reduce_scatter x1, waiting for transfers between devices, on_device(): lax.psum_scatter(grad_w_in, 'dp', scatter_dimension=0, tiled=True)  54.8 us
    psum x1, blocking collectives, on_device(): lax.psum((widen(grad_b_query_part, b_query.shape[0]), widen(grad_b_value_...  41.4 us
    reduce_scatter x1, waiting for transfers between devices, on_device(): lax.psum_scatter(grad_w_value, 'dp', scatter_dimension=0, tiled=True)  37.3 us
    reduce_scatter x1, waiting for transfers between devices, on_device(): lax.psum_scatter(grad_w_out, 'dp', scatter_dimension=1, tiled=True)  36.2 us
    reduce_scatter x1, waiting for transfers between devices, on_device(): lax.psum_scatter((query_part + key_part + value_part).astype(jnp.bfloat16...  27.8 us
    reduce_scatter x1, waiting for transfers between devices, on_device(): lax.psum_scatter(matmul_plain(activation, mat_back).astype(jnp.bfloat16),...  27.4 us
    reduce_scatter x1, waiting for transfers between devices, on_device(): lax.psum_scatter(matmul_plain(context, mat_out).astype(jnp.bfloat16), 'te...  27.1 us
  transfers between devices with their start and end apart: 16, of which 13 were waited for; matrix products, arithmetic and copies ran while one was open for 6% of the time, Pallas kernels for 0%

commit v1 on v0

--- a/solution.py
+++ b/solution.py
@@ -6,6 +6,27 @@
 HD = 64
 epsilon = 1e-06
 masked_value = -1e30
+
+
+def search_frames_for(mat, k_dim):
+    then = list(mat.shape[1:])
+    then[k_dim] *= mat.shape[0]
+    return jnp.moveaxis(mat, 0, k_dim).reshape(then)
+
+
+def bring_cycles(field_in, axis_name):
+    q_n = jax.lax.axis_size(axis_name)
+    o_now = field_in[None]
+    for nth in range(q_n.bit_length() - 1):
+        field_out = 1 << nth
+        sides = []
+        for ii in range(q_n):
+            sides.append((ii, ii ^ field_out))
+        local_now = jax.lax.ppermute(o_now, axis_name=axis_name, perm=sides)
+        part_next = jnp.stack([o_now, local_now])
+        top = jax.lax.axis_index(axis_name) >> nth & 1
+        o_now = jnp.where(top == 0, part_next, part_next[::-1]).reshape(-1, *field_in.shape)
+    return o_now
 
 
 def matmul_plain(left_side, right_side):
@@ -188,6 +209,10 @@
     shift_ffn,
     cotangent,
 ):
+
+    def windows_perform(body, piece_in, along_dim):
+        return search_frames_for(bring_cycles(body, piece_in), along_dim)
+
     tensor_size = lax.axis_size("tensor")
     tensor_index = lax.axis_index("tensor")
     local_rows = tokens.shape[0]
@@ -278,7 +303,7 @@
     grad_shift_attn = jnp.sum(grad_one_out, axis=0)
     grad_one = norm_back(grad_one_out, normed_one, inv_one, gain_attn)
     grad_b_out = jnp.sum(grad_one, axis=0)
-    grad_one_full = lax.all_gather(grad_one.astype(jnp.bfloat16), "tensor", axis=0, tiled=True)
+    grad_one_full = windows_perform(grad_one.astype(jnp.bfloat16), "tensor", 0)
     grad_w_out = matmul_over_rows(context, grad_one_full)
     grad_context = matmul_over_cols(grad_one_full, mat_out).astype(jnp.bfloat16)
     grad_query, grad_keys, grad_values = attend_backward(

time: 600 us -> 604 us (level)
  waiting for transfers between devices: 409 us -> 416 us
    ppermute x0 -> x2, waiting for transfers between devices: none -> 30.9 us  [bring_cycles(): local_now = jax.lax.ppermute(o_now, axis_name=axis_name, perm=sides)]
    all_gather x1 -> x0, waiting for transfers between devices: 26.5 us -> none  [on_device(): lax.all_gather(grad_one.astype(jnp.bfloat16), 'tensor', axis=0, tiled=True)]
  transfers between devices with their start and end apart: 16 -> 17, of which waited for: 13 -> 14; matrix products, arithmetic and copies ran while one was open for 6% -> 6% of each run, Pallas kernels for 0% -> 0%
where the time goes in v1:
time: 604 us; the launch traced here: 603 us
  waiting for transfers between devices  416 us (69%)
  blocking collectives  80.1 us (13%)
  matrix products  47.5 us (8%)
  other arithmetic  21.1 us (3%)
  local copies, waits for them, and re-layouts  18.6 us (3%)
  between operations  17.1 us (3%)
    reduce_scatter x1, waiting for transfers between devices, on_device(): lax.psum_scatter(grad_w_in, 'dp', scatter_dimension=0, tiled=True)  55 us
    reduce_scatter x1, waiting for transfers between devices, on_device(): lax.psum_scatter(grad_w_back, 'dp', scatter_dimension=1, tiled=True)  54.7 us
    psum x1, blocking collectives, on_device(): lax.psum((widen(grad_b_query_part, b_query.shape[0]), widen(grad_b_value_...  39.2 us
    reduce_scatter x1, waiting for transfers between devices, on_device(): lax.psum_scatter(grad_w_value, 'dp', scatter_dimension=0, tiled=True)  37.5 us
    reduce_scatter x1, waiting for transfers between devices, on_device(): lax.psum_scatter(grad_w_out, 'dp', scatter_dimension=1, tiled=True)  36.2 us
    ppermute x2, waiting for transfers between devices, bring_cycles(): local_now = jax.lax.ppermute(o_now, axis_name=axis_name, perm=sides)  30.9 us
    reduce_scatter x1, waiting for transfers between devices, on_device(): lax.psum_scatter((query_part + key_part + value_part).astype(jnp.bfloat16...  27.7 us
    reduce_scatter x1, waiting for transfers between devices, on_device(): lax.psum_scatter(matmul_plain(activation, mat_back).astype(jnp.bfloat16),...  27.4 us
  transfers between devices with their start and end apart: 17, of which 14 were waited for; matrix products, arithmetic and copies ran while one was open for 6% of the time, Pallas kernels for 0%

profile of v1, /device:TPU:0, one launch (start us, length us, event | category | flops | bytes accessed | tf_op | source)
XLA Modules:
  0.0 603.0 jit_solution(1646159791712587952)
XLA Ops:
  13.0 11.6 %all_gather.34 = bf16[1024,256]{1,0:T(8,128)(2,1)S(1)} all-gather(bf16[128,256]{1,0:T(8,128)(2,1)} %param.27), channel_id=1, replica_groups=mesh['dp'=8,'tensor'=4] {'dp'}, dimensions={0}, use_global_device_ids=true | all-gather | bytes 589824 | tf_op jit(solution)/shard_map/all_gather | solution.py:235
  24.6 9.5 %all_gather.35 = bf16[1024,256]{1,0:T(8,128)(2,1)S(1)} all-gather(bf16[128,256]{1,0:T(8,128)(2,1)} %param.24), channel_id=1, replica_groups=mesh['dp'=8,'tensor'=4] {'dp'}, dimensions={0}, use_global_device_ids=true | all-gather | bytes 589824 | tf_op jit(solution)/shard_map/all_gather | solution.py:233
  34.1 9.2 %all_gather.36 = bf16[1024,256]{1,0:T(8,128)(2,1)S(1)} all-gather(bf16[128,256]{1,0:T(8,128)(2,1)} %param.26), channel_id=1, replica_groups=mesh['dp'=8,'tensor'=4] {'dp'}, dimensions={0}, use_global_device_ids=true | all-gather | bytes 589824 | tf_op jit(solution)/shard_map/all_gather | solution.py:234
  43.3 10.6 %all_gather.37 = bf16[256,1024]{1,0:T(8,128)(2,1)} all-gather(bf16[256,128]{1,0:T(8,128)(2,1)S(1)} %copy-done.34), channel_id=1, replica_groups=mesh['dp'=8,'tensor'=4] {'dp'}, dimensions={1}, use_global_device_ids=true | all-gather | bytes 589824 | tf_op jit(solution)/shard_map/all_gather | solution.py:236
  57.1 4.8 while.38
  61.9 2.5 convolution_convert_fusion.3
  65.0 27.1 %reduce-scatter.11.cloned.1.call-done = bf16[128,1024]{1,0:T(8,128)(2,1)} async-done(((bf16[512,1024]{1,0:T(8,128)(2,1)}), bf16[128,1024]{1,0:T(8,128)(2,1)}) %reduce-scatter.11.cloned.1.call-update) | async-done | bytes 262160 | tf_op jit(solution)/shard_map/reduce_scatter | solution.py:246
  94.4 1.8 fusion.21
  97.6 27.1 %all-gather.8.cloned.1.call-done = bf16[512,1024]{1,0:T(8,128)(2,1)} async-done(((bf16[128,1024]{1,0:T(8,128)(2,1)}), bf16[512,1024]{1,0:T(8,128)(2,1)}) %all-gather.8.cloned.1.call-update) | async-done | bytes 1048592 | tf_op jit(solution)/shard_map/all_gather | solution.py:255
  124.7 4.6 multiply_convert_fusion.1
  129.3 24.4 %all-gather.12.cloned.1.call-done = bf16[1024,1024]{1,0:T(8,128)(2,1)} async-done(((bf16[1024,128]{1,0:T(8,128)(2,1)}), bf16[1024,1024]{1,0:T(8,128)(2,1)}) %all-gather.12.cloned.1.call-update) | async-done | bytes 2097168 | tf_op jit(solution)/shard_map/all_gather | solution.py:258
  153.8 3.9 convolution_convert_fusion.2
  157.7 27.4 %reduce-scatter.13.cloned.1.call-done = bf16[128,1024]{1,0:T(8,128)(2,1)} async-done(((bf16[512,1024]{1,0:T(8,128)(2,1)}), bf16[128,1024]{1,0:T(8,128)(2,1)}) %reduce-scatter.13.cloned.1.call-update) | async-done | bytes 262160 | tf_op jit(solution)/shard_map/reduce_scatter | solution.py:264
  188.3 26.4 %all-gather.14.cloned.1.call-done = bf16[512,1024]{1,0:T(8,128)(2,1)} async-done(((bf16[128,1024]{1,0:T(8,128)(2,1)}), bf16[512,1024]{1,0:T(8,128)(2,1)}) %all-gather.14.cloned.1.call-update) | async-done | bytes 1048592 | tf_op jit(solution)/shard_map/all_gather | solution.py:286
  214.7 5.2 fusion.39
  220.9 2.3 convolution_convert_fusion.1
  223.3 26.8 %reduce-scatter.15.cloned.1.call-done = bf16[128,1024]{1,0:T(8,128)(2,1)} async-done(((bf16[512,1024]{1,0:T(8,128)(2,1)}), bf16[128,1024]{1,0:T(8,128)(2,1)}) %reduce-scatter.15.cloned.1.call-update) | async-done | bytes 262160 | tf_op jit(solution)/shard_map/reduce_scatter | solution.py:292
  250.1 1.9 multiply_reduce_fusion.1
  252.0 1.8 fusion.34
  253.9 7.6 %collective-permute-done = bf16[1,128,1024]{2,1,0:T(8,128)(2,1)S(1)} collective-permute-done((bf16[1,128,1024]{2,1,0:T(8,128)(2,1)S(1)}, bf16[1,128,1024]{2,1,0:T(8,128)(2,1)S(1)}, u32[]{:S(2)}, u32[]{:S(2)}) %collective-permute-start) | collective-permute-done | bytes 262176 | tf_op jit(solution)/shard_map/ppermute | solution.py:25
  263.1 23.3 %collective-permute-done.1 = bf16[2,128,1024]{2,1,0:T(8,128)(2,1)S(1)} collective-permute-done((bf16[2,128,1024]{2,1,0:T(8,128)(2,1)S(1)}, bf16[2,128,1024]{2,1,0:T(8,128)(2,1)S(1)}, u32[]{:S(2)}, u32[]{:S(2)}) %collective-permute-start.1) | collective-permute-done | bytes 524320 | tf_op jit(solution)/shard_map/ppermute | solution.py:25
  289.7 13.1 %while.39 = (s32[]{:T(128)}, f32[512,256]{0,1:T(8,128)}, f32[512,256]{0,1:T(8,128)S(1)}, f32[512,256]{0,1:T(8,128)S(1)}, bf16[512,256]{0,1:T(8,128)(2,1)S(1)}, /...) while((s32[]{:T(128)}, f32[512,256]{0,1:T(8,128)}, ...), condition=%wide.region_17.18_spmd.clone, body=%wide.region_15.17_spmd.clone.sunk | while | flops 340395520 | bytes 25846364 | solution.py:189
  302.8 2.9 convolution_bitcast_fusion.2
  314.5 4.5 fusion.43
  320.5 3.3 fusion.15
  326.4 39.2 %all-reduce = (f32[1024]{0:T(1024)}, f32[1024]{0:T(1024)}, f32[1024]{0:T(1024)}, f32[1024]{0:T(1024)}, f32[1024]{0:T(1024)}, /*index=5*/f32[4096]{0:T(1024)}, f32[1024]{0:T(1024)}, f32[1024]{0:T(1024)}, f32[1024]{0:T(1024)}) all-reduce(f32[1024]{0:T(1024)S(1)} %dynamic_update_slice.62, ...), channel_id=1, replica_groups=mesh['dp'=8,'tensor'=4] {'dp','tensor'}, use_global_device_ids=true, to_apply=%region_21.22 | all-reduce | flops 12288 | bytes 98304 | tf_op jit(solution)/shard_map/psum | solution.py:341
  367.3 12.4 %reduce-scatter.21.cloned.1.call-done = f32[128,256]{0,1:T(8,128)} async-done(((f32[1024,256]{0,1:T(8,128)}), f32[128,256]{0,1:T(8,128)}) %reduce-scatter.21.cloned.1.call-update) | async-done | bytes 131088 | tf_op jit(solution)/shard_map/reduce_scatter | solution.py:331
  381.3 37.5 %reduce-scatter.23.cloned.1.call-done = f32[128,256]{0,1:T(8,128)} async-done(((f32[1024,256]{0,1:T(8,128)}), f32[128,256]{0,1:T(8,128)}) %reduce-scatter.23.cloned.1.call-update) | async-done | bytes 131088 | tf_op jit(solution)/shard_map/reduce_scatter | solution.py:332
  420.4 27.7 %reduce-scatter.17.cloned.1.call-done = bf16[128,1024]{1,0:T(8,128)(2,1)} async-done(((bf16[512,1024]{1,0:T(8,128)(2,1)}), bf16[128,1024]{1,0:T(8,128)(2,1)}) %reduce-scatter.17.cloned.1.call-update) | async-done | bytes 262160 | tf_op jit(solution)/shard_map/reduce_scatter | solution.py:323
  450.0 36.2 %reduce-scatter.25.cloned.1.call-done = f32[256,128]{1,0:T(8,128)} async-done(((f32[256,1024]{1,0:T(8,128)}), f32[256,128]{1,0:T(8,128)}) %reduce-scatter.25.cloned.1.call-update) | async-done | bytes 131088 | tf_op jit(solution)/shard_map/reduce_scatter | solution.py:333
  486.2 54.7 %reduce-scatter.29.cloned.1.call-done = f32[1024,128]{1,0:T(8,128)} async-done(((f32[1024,1024]{1,0:T(8,128)}), f32[1024,128]{1,0:T(8,128)}) %reduce-scatter.29.cloned.1.call-update) | async-done | bytes 524304 | tf_op jit(solution)/shard_map/reduce_scatter | solution.py:300
  540.9 55.0 %reduce-scatter.27.cloned.1.call-done = f32[128,1024]{1,0:T(8,128)} async-done(((f32[1024,1024]{1,0:T(8,128)}), f32[128,1024]{1,0:T(8,128)}) %reduce-scatter.27.cloned.1.call-update) | async-done | bytes 524304 | tf_op jit(solution)/shard_map/reduce_scatter | solution.py:299
  (250 shorter events, 56.8 us)
Async XLA Ops:
  8.0 35.3 %copy-start.34 = (bf16[256,128]{1,0:T(8,128)(2,1)S(1)}, bf16[256,128]{1,0:T(8,128)(2,1)}, u32[]{:S(2)}) copy-start(bf16[256,128]{1,0:T(8,128)(2,1)} %param.29) | copy-start | bytes 196612
  8.0 45.8 %all-gather.6.cloned.1.call-start = ((), (), s32[]{:S(2)}) async-start(), calls=%async_computation.10 | async-start | bytes 1310720 | tf_op jit(solution)/shard_map/all_gather | solution.py:231
  8.8 83.4 %reduce-scatter.11.cloned.1.call-start = ((), (), s32[]{:S(2)}) async-start(), calls=%async_computation.11 | async-start | bytes 1310720 | tf_op jit(solution)/shard_map/reduce_scatter | solution.py:246
  24.6 31.2 %copy-start.18 = (bf16[1024,256]{1,0:T(8,128)(2,1)}, bf16[1024,256]{1,0:T(8,128)(2,1)S(1)}, u32[]{:S(2)}) copy-start(bf16[1024,256]{1,0:T(8,128)(2,1)S(1)} %all_gather.34) | copy-start | bytes 1572868
  34.1 22.2 %copy-start.21 = (bf16[1024,256]{1,0:T(8,128)(2,1)}, bf16[1024,256]{1,0:T(8,128)(2,1)S(1)}, u32[]{:S(2)}) copy-start(bf16[1024,256]{1,0:T(8,128)(2,1)S(1)} %all_gather.35) | copy-start | bytes 1572868
  61.8 30.3 %copy-start.2 = (bf16[128,1024]{1,0:T(8,128)(2,1)S(1)}, bf16[128,1024]{1,0:T(8,128)(2,1)}, u32[]{:S(2)}) copy-start(bf16[128,1024]{1,0:T(8,128)(2,1)} %param.22) | copy-start | bytes 786436
  61.9 30.3 %copy-start.32 = (f32[1024]{0:T(1024)S(1)}, f32[1024]{0:T(1024)}, u32[]{:S(2)}) copy-start(f32[1024]{0:T(1024)} %param.30) | copy-start | bytes 12292
  61.9 32.6 %copy-start.33 = (f32[1024]{0:T(1024)S(1)}, f32[1024]{0:T(1024)}, u32[]{:S(2)}) copy-start(f32[1024]{0:T(1024)} %param.31) | copy-start | bytes 12292
  61.9 32.6 %copy-start.35 = (f32[1024]{0:T(1024)S(1)}, f32[1024]{0:T(1024)}, u32[]{:S(2)}) copy-start(f32[1024]{0:T(1024)} %param.32) | copy-start | bytes 12292
  64.4 33.2 %all-gather.10.cloned.1.call-start = ((), (), s32[]{:S(2)}) async-start(), calls=%async_computation.13 | async-start | bytes 2359296 | tf_op jit(solution)/shard_map/all_gather | solution.py:257
  65.0 59.7 %all-gather.8.cloned.1.call-start = ((), (), s32[]{:S(2)}) async-start(), calls=%async_computation.12 | async-start | bytes 1310720 | tf_op jit(solution)/shard_map/all_gather | solution.py:255
  96.3 57.5 %all-gather.12.cloned.1.call-start = ((), (), s32[]{:S(2)}) async-start(), calls=%async_computation.14 | async-start | bytes 2359296 | tf_op jit(solution)/shard_map/all_gather | solution.py:258
  96.9 88.2 %reduce-scatter.13.cloned.1.call-start = ((), (), s32[]{:S(2)}) async-start(), calls=%async_computation.15 | async-start | bytes 1310720 | tf_op jit(solution)/shard_map/reduce_scatter | solution.py:264
  129.3 28.3 %copy-start.27 = (bf16[512,1024]{1,0:T(8,128)(2,1)}, bf16[512,1024]{1,0:T(8,128)(2,1)S(1)}, u32[]{:S(2)}) copy-start(bf16[512,1024]{1,0:T(8,128)(2,1)S(1)} %get-tuple-element.633) | copy-start | bytes 3145732
  153.7 31.4 %copy-start.11 = (bf16[128,1024]{1,0:T(8,128)(2,1)S(1)}, bf16[128,1024]{1,0:T(8,128)(2,1)}, u32[]{:S(2)}) copy-start(bf16[128,1024]{1,0:T(8,128)(2,1)} %reduce-scatter.11.cloned.1.call-done) | copy-start | bytes 786436
  153.8 31.4 %copy-start.41 = (f32[1024]{0:T(1024)S(1)}, f32[1024]{0:T(1024)}, u32[]{:S(2)}) copy-start(f32[1024]{0:T(1024)} %param.36) | copy-start | bytes 12292
  157.6 29.0 %copy-start.29 = (bf16[128,1024]{1,0:T(8,128)(2,1)S(1)}, bf16[128,1024]{1,0:T(8,128)(2,1)}, u32[]{:S(2)}) copy-start(bf16[128,1024]{1,0:T(8,128)(2,1)} %param.39) | copy-start | bytes 786436
  157.6 29.0 %copy-start.36 = (f32[1024]{0:T(1024)S(1)}, f32[1024]{0:T(1024)}, u32[]{:S(2)}) copy-start(f32[1024]{0:T(1024)} %param.37) | copy-start | bytes 12292
  157.6 29.4 %copy-start.42 = (f32[1024]{0:T(1024)S(1)}, f32[1024]{0:T(1024)}, u32[]{:S(2)}) copy-start(f32[1024]{0:T(1024)} %param.38) | copy-start | bytes 12292
  157.7 57.1 %all-gather.14.cloned.1.call-start = ((), (), s32[]{:S(2)}) async-start(), calls=%async_computation.16 | async-start | bytes 1310720 | tf_op jit(solution)/shard_map/all_gather | solution.py:286
  188.1 62.0 %reduce-scatter.15.cloned.1.call-start = ((), (), s32[]{:S(2)}) async-start(), calls=%async_computation.17 | async-start | bytes 1310720 | tf_op jit(solution)/shard_map/reduce_scatter | solution.py:292
  223.2 142.4 %reduce-scatter.19.cloned.1.call-start = ((), (), s32[]{:S(2)}) async-start(), calls=%async_computation.19 | async-start | bytes 1179648 | tf_op jit(solution)/shard_map/reduce_scatter | solution.py:330
  253.8 32.7 %copy-start.14 = (f32[128,1024]{1,0:T(8,128)}, f32[128,1024]{1,0:T(8,128)S(1)}, u32[]{:S(2)}) copy-start(f32[128,1024]{1,0:T(8,128)S(1)} %get-tuple-element.615) | copy-start | bytes 1572868
  253.9 7.7 %collective-permute-start = (bf16[1,128,1024]{2,1,0:T(8,128)(2,1)S(1)}, bf16[1,128,1024]{2,1,0:T(8,128)(2,1)S(1)}, u32[]{:S(2)}, u32[]{:S(2)}) collective-permute-start(bf16[1,128,1024]{2,1,0:T(8,128)(2,1)S(1)} %get-tuple-element.630), channel_id=1, source_target_pairs={{0,1},{1,0},{2,3},{3,2},{4,5},{5,4},{6,7},{7,6},{8,9},{9,8},{10,11... | collective-permute-start | bytes 786440 | tf_op jit(solution)/shard_map/ppermute | solution.py:25
  261.8 24.6 %collective-permute-start.1 = (bf16[2,128,1024]{2,1,0:T(8,128)(2,1)S(1)}, bf16[2,128,1024]{2,1,0:T(8,128)(2,1)S(1)}, u32[]{:S(2)}, u32[]{:S(2)}) collective-permute-start(bf16[2,128,1024]{2,1,0:T(8,128)(2,1)S(1)} %get-tuple-element.628), channel_id=1, source_target_pairs={{0,2},{1,3},{2,0},{3,1},{4,6},{5,7},{6,4},{7,5},{8,10},{9,11},{10,... | collective-permute-start | bytes 1572872 | tf_op jit(solution)/shard_map/ppermute | solution.py:25
  305.7 74.0 %reduce-scatter.21.cloned.1.call-start = ((), (), s32[]{:S(2)}) async-start(), calls=%async_computation.20 | async-start | bytes 1179648 | tf_op jit(solution)/shard_map/reduce_scatter | solution.py:331
  307.2 111.6 %reduce-scatter.23.cloned.1.call-start = ((), (), s32[]{:S(2)}) async-start(), calls=%async_computation.21 | async-start | bytes 1179648 | tf_op jit(solution)/shard_map/reduce_scatter | solution.py:332
  308.8 139.4 %reduce-scatter.17.cloned.1.call-start = ((), (), s32[]{:S(2)}) async-start(), calls=%async_computation.18 | async-start | bytes 1310720 | tf_op jit(solution)/shard_map/reduce_scatter | solution.py:323
  312.9 173.3 %reduce-scatter.25.cloned.1.call-start = ((), (), s32[]{:S(2)}) async-start(), calls=%async_computation.22 | async-start | bytes 1179648 | tf_op jit(solution)/shard_map/reduce_scatter | solution.py:333
  314.4 226.5 %reduce-scatter.29.cloned.1.call-start = ((), (), s32[]{:S(2)}) async-start(), calls=%async_computation.24 | async-start | bytes 4718592 | tf_op jit(solution)/shard_map/reduce_scatter | solution.py:300
  319.0 276.9 %reduce-scatter.27.cloned.1.call-start = ((), (), s32[]{:S(2)}) async-start(), calls=%async_computation.23 | async-start | bytes 4718592 | tf_op jit(solution)/shard_map/reduce_scatter | solution.py:299
  323.8 124.4 %copy-start.15 = (f32[128,1024]{1,0:T(8,128)S(1)}, f32[128,1024]{1,0:T(8,128)}, u32[]{:S(2)}) copy-start(f32[128,1024]{1,0:T(8,128)} %copy-done.14) | copy-start | bytes 1572868
  (41 other events, 81.2 us)
Sparse Core Ops, SparseCore 0:
  10.4 30.6 all-gather.5
  64.5 27.5 reduce-scatter.10
  157.8 27.2 reduce-scatter.12
  188.2 26.4 all-gather.13
  223.3 26.6 reduce-scatter.14
Sparse Core Ops, SparseCore 1:
  66.8 27.9 all-gather.9
  96.7 27.9 all-gather.7
  126.4 27.3 all-gather.11
  305.8 34.7 reduce-scatter.18
  343.8 35.8 reduce-scatter.20
  382.8 35.9 reduce-scatter.22
  420.9 27.2 reduce-scatter.16
  451.8 34.3 reduce-scatter.24
  490.0 50.9 reduce-scatter.28
  544.9 51.0 reduce-scatter.26
